TPU v7x, 32 devices: a whole 2x2x4 slice. The times are simulated.
32 devices in a mesh: gx: 8 (over y, x, core), yz: 4 (over z).
Axes of the slice: x: 2, y: 2, z: 4, core: 2. Of those that a mesh axis runs over, the one named last changes fastest.
Arguments:
- spectra: bfloat16 [2, 20, 640, 16, 512], P(None, None, None, 'gx', 'yz'), may hold values from -6 to 6
- kernel_mesh: float32 [20], replicated, may hold values from 0.02 to 6, as said below
- density: float32 [640, 16, 512], P('gx', None, 'yz'), may hold values from 0.05 to 1
- local_wave: float32 [640, 16, 512], P('gx', None, 'yz'), may hold values from 0.15 to 4.8
- wave_density: float32 [640, 16, 512], P('gx', None, 'yz'), may hold values from -1.2 to 1.2
- wave_gradient: float32 [3, 640, 16, 512], P(None, 'gx', None, 'yz'), may hold values from -0.6 to 0.6
Outputs:
- potential: float32 [640, 16, 512], P('gx', None, 'yz')
Inputs may be any that keep to these rules, and one draw needn't show every extreme that they name: `kernel_mesh`: strictly increasing; entry 0 is at most 0.1 and entry 19 at least 5.0.
All inputs are finite; a program needn't handle non-finite values.
Results may differ from a plain program's by a relative error of at most 0.0033.
Values sent between devices are 32-bit elements.
A program may use at most 192 MiB of HBM per device.

v0:
```python
import math

import jax
import jax.numpy as jnp
from jax import lax
from jax.sharding import PartitionSpec as P


def extended(block, sides, width):
    for axis, dim in sides:
        count = lax.axis_size(axis)
        forward = [(i, i + 1) for i in range(count - 1)]
        forward.append((count - 1, 0))
        backward = [(target, source) for source, target in forward]
        low = lax.ppermute(
            lax.slice_in_dim(block, block.shape[dim] - width, None, axis=dim), axis, forward
        )
        high = lax.ppermute(lax.slice_in_dim(block, 0, width, axis=dim), axis, backward)
        block = jnp.concatenate([low, block, high], axis=dim)
    return block


def dft_tables(length):
    rows_index = lax.broadcasted_iota(jnp.int32, (length, length), 0)
    cols_index = lax.broadcasted_iota(jnp.int32, (length, length), 1)
    phases = rows_index * cols_index % length
    angles = phases.astype(jnp.float32) * (2.0 * math.pi / length)
    return jnp.stack([jnp.cos(angles), -jnp.sin(angles)]).astype(jnp.bfloat16)


def spline_second(kernel_mesh):
    points = kernel_mesh.shape[0]
    spacing = kernel_mesh[1:] - kernel_mesh[:-1]
    identity = jnp.eye(points, dtype=jnp.float32)
    right_side = (identity[2:] - identity[1:-1]) / spacing[1:, None] - (
        identity[1:-1] - identity[:-2]
    ) / spacing[:-1, None]
    zero_entry = jnp.zeros((1,), jnp.float32)
    lower_band = jnp.concatenate([zero_entry, spacing[1:-1] / 6.0])
    main_band = (spacing[:-1] + spacing[1:]) / 3.0
    upper_band = jnp.concatenate([spacing[1:-1] / 6.0, zero_entry])
    interior = lax.linalg.tridiagonal_solve(lower_band, main_band, upper_band, right_side)
    border = jnp.zeros((1, points), jnp.float32)
    return jnp.concatenate([border, interior, border])


def basis_terms(weight_a, weight_b, span_width, lower_hot, upper_hot, second_lower, second_upper):
    basis_value = (
        weight_a * lower_hot
        + weight_b * upper_hot
        + (weight_a * weight_a * weight_a - weight_a) * span_width * span_width / 6.0 * second_lower
        + (weight_b * weight_b * weight_b - weight_b) * span_width * span_width / 6.0 * second_upper
    )
    basis_slope = (
        (upper_hot - lower_hot) / span_width
        - (3.0 * weight_a * weight_a - 1.0) * span_width / 6.0 * second_lower
        + (3.0 * weight_b * weight_b - 1.0) * span_width / 6.0 * second_upper
    )
    return (basis_value, basis_slope)


def contract(components, local_wave, kernel_mesh, second):
    points = kernel_mesh.shape[0]
    interval = jnp.zeros(local_wave.shape, jnp.int32)
    for index in range(1, points - 1):
        interval = interval + (local_wave >= kernel_mesh[index]).astype(jnp.int32)
    labels = lax.broadcasted_iota(jnp.int32, (points, 1, 1, 1), 0)
    lower_hot = (labels == interval[None]).astype(jnp.float32)
    upper_hot = (labels == interval[None] + 1).astype(jnp.float32)
    column = kernel_mesh.reshape((points, 1, 1, 1))
    lower_point = jnp.sum(lower_hot * column, axis=0)
    finish_point = jnp.sum(upper_hot * column, axis=0)
    span_width = finish_point - lower_point
    weight_a = (finish_point - local_wave) / span_width
    weight_b = (local_wave - lower_point) / span_width
    second_lower = jnp.einsum("ba,bxyz->axyz", second, lower_hot, precision=lax.Precision.HIGHEST)
    second_upper = jnp.einsum("ba,bxyz->axyz", second, upper_hot, precision=lax.Precision.HIGHEST)
    basis_value, basis_slope = basis_terms(
        weight_a, weight_b, span_width, lower_hot, upper_hot, second_lower, second_upper
    )
    return (jnp.sum(components * basis_value, axis=0), jnp.sum(components * basis_slope, axis=0))


def shards(spectra, kernel_mesh, density, local_wave, wave_density, wave_gradient):
    length = spectra.shape[2]
    tables = dft_tables(length)
    accumulated = jnp.einsum("pckyz,pkx->cxyz", spectra, tables, preferred_element_type=jnp.float32)
    components = accumulated * length ** (-0.5)
    second = spline_second(kernel_mesh)
    slab_density, slab_wave, slab_rate = (
        lax.all_to_all(density, "gx", split_axis=1, concat_axis=0, tiled=True),
        lax.all_to_all(local_wave, "gx", split_axis=1, concat_axis=0, tiled=True),
        lax.all_to_all(wave_density, "gx", split_axis=1, concat_axis=0, tiled=True),
    )
    sum_value, sum_slope = contract(components, slab_wave, kernel_mesh, second)
    slab_local = sum_value + slab_density * slab_rate * sum_slope
    slab_scale = slab_density * sum_slope
    local_term, grad_scale = (
        lax.all_to_all(slab_local, "gx", split_axis=0, concat_axis=1, tiled=True),
        lax.all_to_all(slab_scale, "gx", split_axis=0, concat_axis=1, tiled=True),
    )
    flux_first = grad_scale * wave_gradient[0]
    flux_second = grad_scale * wave_gradient[1]
    flux_third = grad_scale * wave_gradient[2]
    padded_first = extended(flux_first, (("gx", 0),), 1)
    padded_third = extended(flux_third, (("yz", 2),), 1)
    divergence = 0.5 * (padded_first[2:] - padded_first[:-2])
    divergence = divergence + 0.5 * (jnp.roll(flux_second, -1, 1) - jnp.roll(flux_second, 1, 1))
    divergence = divergence + 0.5 * (padded_third[:, :, 2:] - padded_third[:, :, :-2])
    return local_term - divergence


def solution(mesh):
    return jax.shard_map(
        shards,
        mesh=mesh,
        in_specs=(
            P(None, None, None, "gx", "yz"),
            P(),
            P("gx", None, "yz"),
            P("gx", None, "yz"),
            P("gx", None, "yz"),
            P(None, "gx", None, "yz"),
        ),
        out_specs=P("gx", None, "yz"),
        check_vma=False,
    )
```

profile of v0, /device:TPU:0, one launch (start us, length us, event | category | flops | bytes accessed | tf_op | source)
XLA Modules:
  0.0 220.2 jit_solution(14158756007778748389)
XLA Ops:
  0.0 2.1 copy.69
  2.1 5.2 %all-to-all-start = ((f32[80,16,128]{2,0,1:T(8,128)}), f32[80,16,128]{2,0,1:T(8,128)S(1)}, u32[]{:S(2)}, u32[]{:S(2)}) async-start(f32[80,16,128]{2,0,1:T(8,128)} %copy.69), calls=%async_computation | async-start | bytes 1310720 | tf_op jit(solution)/shard_map/all_to_all | solution.py:92
  7.3 0.8 slice_subtract_fusion.19
  8.1 0.1 add_multiply_fusion
  8.3 0.7 fusion.83
  9.0 0.7 fusion.84
  40.5 0.1 fusion.37
  40.5 10.6 %fusion.43 = (f32[1,20]{1,0:T(1,128)S(1)}, f32[1,20]{1,0:T(1,128)S(1)}, f32[1,20]{1,0:T(1,128)S(1)}, f32[1,20]{1,0:T(1,128)S(1)}, f32[1,20]{1,0:T(1,128)S(1)}, /...) fusion(f32[18,20]{1,0:T(8,128)S(1)} %fusion.37, ...), kind=kLoop, calls=%fused_computation.98 | loop fusion | flops 980 | bytes 2852 | tf_op jit(solution)/shard_map/eval_jaxpr/div | solution.py:42
  52.5 2.2 copy.77
  54.6 2.1 copy.79
  57.4 0.7 multiply_subtract_fusion.2
  58.1 0.1 concatenate.26
  58.2 2.0 fusion.85
  60.2 7.7 %negate_convert_fusion = (bf16[1,640,640]{1,2,0:T(8,128)(2,1)}, bf16[1,640,640]{1,2,0:T(8,128)(2,1)}) fusion(), kind=kLoop, calls=%fused_computation.21 | loop fusion | flops 4915200 | bytes 1638400 | tf_op jit(solution)/shard_map/convert.1
  67.9 4.2 %all-to-all-start.1 = ((f32[80,16,128]{2,0,1:T(8,128)}), f32[80,16,128]{2,0,1:T(8,128)}, u32[]{:S(2)}, u32[]{:S(2)}) async-start(f32[80,16,128]{2,0,1:T(8,128)} %copy.77), calls=%async_computation.1 | async-start | bytes 1310720 | tf_op jit(solution)/shard_map/all_to_all | solution.py:91
  72.2 12.2 %broadcast_add_fusion = (s32[640,2,128]{2,0,1:T(8,128)S(1)}, s32[640,2,128]{2,0,1:T(8,128)S(1)}) fusion(f32[]{:T(128)} %bitcast.25, f32[]{:T(128)} %bitcast.24, f32[]{:T(128)} %bitcast.23, f32[]{:T(128)} %bitcast.22, f32[]{:T(128)} %bitcast.21, f32[]{:T(128)} %bitcast.20, f32[]{:T(128)} %bitcast.19, f32[]{:T(128)} %bitcast.18, f32[]{:T(128)} %bitcast.17, ...), kind=kLoop, calls=%fused_computation.85 | loop fusion | flops 8847360 | bytes 1966152 | tf_op jit(solution)/shard_map/add | solution.py:69
  84.4 3.5 %select_reduce_fusion = (f32[640,2,128]{2,0,1:T(8,128)S(1)}, f32[640,2,128]{2,0,1:T(8,128)S(1)}) fusion(f32[20]{0:T(128)} %param.7, s32[640,2,128]{2,0,1:T(8,128)S(1)} %get-tuple-element.50, s32[640,2,128]{2,0,1:T(8,128)S(1)} %get-tuple-element.49), kind=kLoop, calls=%fused_computation.11 | loop fusion | flops 19333120 | bytes 2621520 | tf_op jit(solution)/shard_map/reduce_sum | solution.py:71
  87.9 4.4 %iota_compare_fusion = (pred[20,640,2,128]{3,1,2,0:T(32,128)(4,1)S(1)}, pred[20,640,2,128]{3,1,2,0:T(32,128)(4,1)}) fusion(s32[640,2,128]{2,0,1:T(8,128)S(1)} %get-tuple-element.49, s32[640,2,128]{2,0,1:T(8,128)S(1)} %get-tuple-element.50), kind=kLoop, calls=%fused_computation.13 | loop fusion | flops 6553600 | bytes 7864320 | tf_op jit(solution)/shard_map/eq | solution.py:69
  92.4 1.2 fusion.19
  93.6 0.8 copy-done.2
  94.5 1.3 fusion.22
  95.7 4.4 %all-to-all-start.2 = ((f32[80,16,128]{2,0,1:T(8,128)}), f32[80,16,128]{2,0,1:T(8,128)}, u32[]{:S(2)}, u32[]{:S(2)}) async-start(f32[80,16,128]{2,0,1:T(8,128)} %copy.79), calls=%async_computation.2 | async-start | bytes 1310720 | tf_op jit(solution)/shard_map/all_to_all | solution.py:93
  100.1 2.0 copy.78
  102.1 17.0 %fusion.2 = f32[20,640,2,128]{3,0,2,1:T(8,128)} fusion(pred[20,640,2,128]{3,1,2,0:T(32,128)(4,1)} %get-tuple-element.126, f32[20,20]{1,0:T(8,128)S(1)} %concatenate.26), kind=kOutput, calls=%fused_computation.2 | convolution fusion | flops 786432000 | bytes 16385600 | tf_op jit(solution)/shard_map/ba,bxyz->axyz/dot_general | solution.py:76
  119.1 26.9 %fusion = f32[20,640,2,128]{3,0,2,1:T(8,128)} fusion(pred[20,640,2,128]{3,1,2,0:T(32,128)(4,1)S(1)} %get-tuple-element.125, f32[20,20]{1,0:T(8,128)S(1)} %concatenate.26), kind=kOutput, calls=%fused_computation | convolution fusion | flops 786432000 | bytes 16385600 | tf_op jit(solution)/shard_map/ba,bxyz->axyz/dot_general | solution.py:77
  146.1 1.1 copy.80
  147.2 1.8 fusion.15
  148.9 32.3 %fusion.4 = (f32[640,2,128]{2,0,1:T(8,128)S(1)}, f32[640,2,128]{2,0,1:T(8,128)}) fusion(f32[20,640,2,128]{3,0,2,1:T(8,128)} %fusion, f32[20,640,2,128]{3,0,2,1:T(8,128)} %fusion.2, f32[640,2,128]{2,0,1:T(8,128)S(1)} %get-tuple-element.68, f32[640,2,128]{2,0,1:T(8,128)S(1)} %get-tuple-element.67, f32[640,2,128]{2,0,1:T(8,128)} %get-tuple-element.13, ...), kind=kOutput, calls=%fused_computation.6 | convolution fusion | flops 8463646720 | bytes 48168960 | tf_op jit(solution)/shard_map/pckyz,pkx->cxyz/dot_general | solution.py:87
  181.2 1.2 fusion.33
  182.5 1.4 copy.86
  183.8 4.1 %all-to-all-start.4 = ((f32[640,2,128]{2,1,0:T(2,128)}), f32[640,2,128]{2,1,0:T(2,128)S(1)}, u32[]{:S(2)}, u32[]{:S(2)}) async-start(f32[640,2,128]{2,1,0:T(2,128)} %copy.86), calls=%async_computation.4 | async-start | bytes 1310720 | tf_op jit(solution)/shard_map/all_to_all | solution.py:100
  188.0 2.7 %fusion.78 = (f32[1,80,16,128]{3,2,1,0:T(8,128)S(1)}, f32[1,80,16,128]{3,2,1,0:T(8,128)}, f32[1,80,16,128]{3,2,1,0:T(8,128)}) fusion(f32[3,80,16,128]{3,2,1,0:T(8,128)} %param.11), kind=kLoop, calls=%fused_computation.151 | loop fusion | bytes 3932160 | tf_op jit(solution)/shard_map/slice | solution.py:103
  190.7 1.4 copy.83
  192.0 7.1 %all-to-all-done.4 = f32[640,2,128]{2,1,0:T(2,128)S(1)} async-done(((f32[640,2,128]{2,1,0:T(2,128)}), f32[640,2,128]{2,1,0:T(2,128)S(1)}, u32[]{:S(2)}, u32[]{:S(2)}) %all-to-all-start.4) | async-done | bytes 655392 | tf_op jit(solution)/shard_map/all_to_all | solution.py:100
  199.1 3.5 %all-to-all-start.3 = ((f32[640,2,128]{2,1,0:T(2,128)}), f32[640,2,128]{2,1,0:T(2,128)S(1)}, u32[]{:S(2)}, u32[]{:S(2)}) async-start(f32[640,2,128]{2,1,0:T(2,128)} %copy.83), calls=%async_computation.3 | async-start | bytes 1310720 | tf_op jit(solution)/shard_map/all_to_all | solution.py:99
  202.7 1.9 fusion.30
  204.7 1.0 fusion.82
  205.7 1.3 copy.92
  207.0 3.6 %collective-permute-start.2 = (f32[80,16,1]{0,1,2:T(8,128)S(1)}, f32[80,16,1]{0,1,2:T(8,128)S(1)}, u32[]{:S(2)}, u32[]{:S(2)}) collective-permute-start(f32[80,16,1]{0,1,2:T(8,128)S(1)} %copy.92), channel_id=1, source_target_pairs={{1,0},{2,1},{3,2},{0,3},{5,4},{6,5},{7,6},{4,7},{9,8},{10,9},{11,1... | collective-permute-start | bytes 15368 | tf_op jit(solution)/shard_map/ppermute | solution.py:18
  210.7 0.2 copy.94
  210.9 2.3 %collective-permute-start = (f32[1,16,128]{2,0,1:T(1,128)S(1)}, f32[1,16,128]{2,0,1:T(1,128)S(1)}, u32[]{:S(2)}, u32[]{:S(2)}) collective-permute-start(f32[1,16,128]{2,0,1:T(1,128)S(1)} %get-tuple-element.63), channel_id=1, source_target_pairs={{4,0},{8,4},{12,8},{16,12},{20,16},{24,20},{28,24},{0,28},{5,1},{9... | collective-permute-start | bytes 24584 | tf_op jit(solution)/shard_map/ppermute | solution.py:18
  213.3 1.1 fusion.80
  214.5 0.3 copy.93
  214.8 1.5 collective-permute-done.3
  216.4 0.3 copy.95
  216.6 0.6 collective-permute-done.1
  217.3 1.8 fusion.26
  219.1 1.0 copy.96
  (25 shorter events, 0.4 us)
Async XLA Ops:
  2.1 65.8 %all-to-all-start = ((f32[80,16,128]{2,0,1:T(8,128)}), f32[80,16,128]{2,0,1:T(8,128)S(1)}, u32[]{:S(2)}, u32[]{:S(2)}) async-start(f32[80,16,128]{2,0,1:T(8,128)} %copy.69), calls=%async_computation | async-start | bytes 1310720 | tf_op jit(solution)/shard_map/all_to_all | solution.py:92
  67.9 27.8 %all-to-all-start.1 = ((f32[80,16,128]{2,0,1:T(8,128)}), f32[80,16,128]{2,0,1:T(8,128)}, u32[]{:S(2)}, u32[]{:S(2)}) async-start(f32[80,16,128]{2,0,1:T(8,128)} %copy.77), calls=%async_computation.1 | async-start | bytes 1310720 | tf_op jit(solution)/shard_map/all_to_all | solution.py:91
  84.4 3.5 %copy-start = (s32[640,2,128]{2,0,1:T(8,128)}, s32[640,2,128]{2,0,1:T(8,128)S(1)}, u32[]{:S(2)}) copy-start(s32[640,2,128]{2,0,1:T(8,128)S(1)} %get-tuple-element.49) | copy-start | bytes 1966084
  84.4 8.0 %copy-start.1 = (s32[640,2,128]{2,0,1:T(8,128)}, s32[640,2,128]{2,0,1:T(8,128)S(1)}, u32[]{:S(2)}) copy-start(s32[640,2,128]{2,0,1:T(8,128)S(1)} %get-tuple-element.50) | copy-start | bytes 1966084
  93.6 0.8 copy-start.2
  95.7 50.3 %all-to-all-start.2 = ((f32[80,16,128]{2,0,1:T(8,128)}), f32[80,16,128]{2,0,1:T(8,128)}, u32[]{:S(2)}, u32[]{:S(2)}) async-start(f32[80,16,128]{2,0,1:T(8,128)} %copy.79), calls=%async_computation.2 | async-start | bytes 1310720 | tf_op jit(solution)/shard_map/all_to_all | solution.py:93
  148.9 32.3 %copy-start.3 = (f32[8,80,2,128]{3,1,0,2:T(8,128)S(1)}, f32[8,80,2,128]{3,1,0,2:T(8,128)}, u32[]{:S(2)}) copy-start(f32[8,80,2,128]{3,1,0,2:T(8,128)} %copy.78) | copy-start | bytes 1966084
  183.8 15.2 %all-to-all-start.4 = ((f32[640,2,128]{2,1,0:T(2,128)}), f32[640,2,128]{2,1,0:T(2,128)S(1)}, u32[]{:S(2)}, u32[]{:S(2)}) async-start(f32[640,2,128]{2,1,0:T(2,128)} %copy.86), calls=%async_computation.4 | async-start | bytes 1310720 | tf_op jit(solution)/shard_map/all_to_all | solution.py:100
  199.1 15.3 %all-to-all-start.3 = ((f32[640,2,128]{2,1,0:T(2,128)}), f32[640,2,128]{2,1,0:T(2,128)S(1)}, u32[]{:S(2)}, u32[]{:S(2)}) async-start(f32[640,2,128]{2,1,0:T(2,128)} %copy.83), calls=%async_computation.3 | async-start | bytes 1310720 | tf_op jit(solution)/shard_map/all_to_all | solution.py:99
  207.0 7.5 %collective-permute-start.2 = (f32[80,16,1]{0,1,2:T(8,128)S(1)}, f32[80,16,1]{0,1,2:T(8,128)S(1)}, u32[]{:S(2)}, u32[]{:S(2)}) collective-permute-start(f32[80,16,1]{0,1,2:T(8,128)S(1)} %copy.92), channel_id=1, source_target_pairs={{1,0},{2,1},{3,2},{0,3},{5,4},{6,5},{7,6},{4,7},{9,8},{10,9},{11,1... | collective-permute-start | bytes 15368 | tf_op jit(solution)/shard_map/ppermute | solution.py:18
  210.9 5.5 %collective-permute-start.3 = (f32[80,16,1]{0,1,2:T(8,128)S(1)}, f32[80,16,1]{0,1,2:T(8,128)S(1)}, u32[]{:S(2)}, u32[]{:S(2)}) collective-permute-start(f32[80,16,1]{0,1,2:T(8,128)S(1)} %copy.94), channel_id=1, source_target_pairs={{0,1},{1,2},{2,3},{3,0},{4,5},{5,6},{6,7},{7,4},{8,9},{9,10},{10,1... | collective-permute-start | bytes 15368 | tf_op jit(solution)/shard_map/ppermute | solution.py:15
  210.9 5.7 %collective-permute-start = (f32[1,16,128]{2,0,1:T(1,128)S(1)}, f32[1,16,128]{2,0,1:T(1,128)S(1)}, u32[]{:S(2)}, u32[]{:S(2)}) collective-permute-start(f32[1,16,128]{2,0,1:T(1,128)S(1)} %get-tuple-element.63), channel_id=1, source_target_pairs={{4,0},{8,4},{12,8},{16,12},{20,16},{24,20},{28,24},{0,28},{5,1},{9... | collective-permute-start | bytes 24584 | tf_op jit(solution)/shard_map/ppermute | solution.py:18
  213.3 4.0 %collective-permute-start.1 = (f32[1,16,128]{2,0,1:T(1,128)S(1)}, f32[1,16,128]{2,0,1:T(1,128)S(1)}, u32[]{:S(2)}, u32[]{:S(2)}) collective-permute-start(f32[1,16,128]{2,0,1:T(1,128)S(1)} %get-tuple-element.64), channel_id=1, source_target_pairs={{0,4},{4,8},{8,12},{12,16},{16,20},{20,24},{24,28},{28,0},{1,5},{5... | collective-permute-start | bytes 24584 | tf_op jit(solution)/shard_map/ppermute | solution.py:15
where the time goes:
time: 222 us; the launch traced here: 220 us
  matrix products  76.2 us (34%)
  other arithmetic  49.5 us (22%)
  between operations  32.9 us (15%)
  starting transfers between devices  27.5 us (12%)
  local copies, waits for them, and re-layouts  24.8 us (11%)
  waiting for transfers between devices  9.24 us (4%)
    dot_general x1, matrix products, shards(): jnp.einsum('pckyz,pkx->cxyz', spectra, tables, preferred_element_type=jnp...  32.3 us
    dot_general x1, matrix products, contract(): jnp.einsum('ba,bxyz->axyz', second, upper_hot, precision=lax.Precision.HI...  26.9 us
    dot_general x1, matrix products, contract(): jnp.einsum('ba,bxyz->axyz', second, lower_hot, precision=lax.Precision.HI...  17 us
    add x1, other arithmetic, contract(): upper_hot = (labels == interval[None] + 1).astype(jnp.float32)  12.2 us
    div x1, other arithmetic, spline_second(): lax.linalg.tridiagonal_solve(lower_band, main_band, upper_band, right_side)  10.6 us
    another operation x1, other arithmetic  7.68 us
    unnamed x11, local copies, waits for them, and re-layouts  7.29 us
    all_to_all x1, waiting for transfers between devices, shards(): lax.all_to_all(slab_scale, 'gx', split_axis=0, concat_axis=1, tiled=True)  7.07 us
  transfers between devices with their start and end apart: 9, of which 3 were waited for; matrix products, arithmetic and copies ran while one was open for 49% of the time, Pallas kernels for 0%

commit v1 on v0

v1 whole, which is shorter than its diff:
```python
import functools
import math

import jax
import jax.numpy as jnp
import numpy as np
from jax import lax
from jax.experimental import pallas as pl
from jax.experimental.pallas import tpu as pltpu
from jax.sharding import PartitionSpec as P

SUB = 8


def split_tables(length, blocks, padded_rows):
    quarter = length // 4
    per_block = length // blocks // 4
    out = np.zeros((4, blocks, padded_rows, 2, quarter, 2), np.float32)
    k = np.arange(quarter)
    for r in range(4):
        m = np.arange(blocks * per_block).reshape(blocks, per_block)
        x = 4 * m + r
        phases = (x[..., None] * k) % length
        angles = phases.astype(np.float32) * np.float32(2.0 * math.pi / length)
        pair = np.stack([np.cos(angles), -np.sin(angles)], axis=2)
        for y in range(2):
            out[r, :, y : 2 * per_block : 2, :, :, y] = pair
    flat = out.reshape(4, blocks * padded_rows, 4 * quarter)
    return flat.astype(jnp.bfloat16)


def spline_coefficients(mesh_ref, coef_ref):
    points = mesh_ref.shape[0]
    ones = jnp.ones((SUB, 128), jnp.float32)
    node = [ones * mesh_ref[j] for j in range(points)]
    gap = [node[j + 1] - node[j] for j in range(points - 1)]
    carry = jnp.zeros((SUB, 128), jnp.float32)
    for j in range(points):
        coef_ref[0, j] = node[j]
        if j < points - 1:
            coef_ref[1, j] = 1.0 / gap[j]
        if 1 <= j < points - 1:
            pivot = 1.0 / (2.0 * (gap[j - 1] + gap[j]) - gap[j - 1] * carry)
            carry = gap[j] * pivot
            coef_ref[2, j] = pivot
            coef_ref[3, j] = gap[j - 1] * pivot
            coef_ref[4, j] = carry


def spline_sums(wave, value_of, coef_ref, points, scale):
    values = [value_of(j) for j in range(points)]
    forward = [None] * points
    slope_before = (values[1] - values[0]) * coef_ref[1, 0]
    for j in range(1, points - 1):
        slope_here = (values[j + 1] - values[j]) * coef_ref[1, j]
        term = (slope_here - slope_before) * coef_ref[2, j]
        if j > 1:
            term = term - coef_ref[3, j] * forward[j - 1]
        forward[j] = term
        slope_before = slope_here
    zero = jnp.zeros_like(wave)
    sixth = [zero] * points
    for j in range(points - 2, 0, -1):
        sixth[j] = forward[j] if j == points - 2 else forward[j] - coef_ref[4, j] * sixth[j + 1]
    picked = [values[0], values[1], sixth[0], sixth[1], coef_ref[0, 0], coef_ref[0, 1]]
    for j in range(1, points - 1):
        above = wave >= coef_ref[0, j]
        here = [values[j], values[j + 1], sixth[j], sixth[j + 1], coef_ref[0, j], coef_ref[0, j + 1]]
        picked = [jnp.where(above, new, old) for new, old in zip(here, picked)]
    value_low, value_high, sixth_low, sixth_high, low, high = picked
    width = high - low
    inverse = 1.0 / width
    a = (high - wave) * inverse
    b = (wave - low) * inverse
    square_a, square_b = a * a, b * b
    bent = ((square_a * a - a) * sixth_low + (square_b * b - b) * sixth_high) * (width * width)
    total = a * value_low + b * value_high + bent
    turn = ((3.0 * square_b - 1.0) * sixth_high - (3.0 * square_a - 1.0) * sixth_low) * width
    slope = (value_high - value_low) * inverse + turn
    return total * scale, slope * scale


def slab_kernel(blocks, padded, mesh_ref, spectra_ref, table_ref, wave_ref, out_ref, folded, comps, coef):
    step = pl.program_id(0)
    points = mesh_ref.shape[0]
    quarter_rows = spectra_ref.shape[3]
    chunk = 32
    for which in range(2):
        lanes = slice(which * 128, which * 128 + 128)

        @pl.loop(0, quarter_rows // chunk)
        def _(c):
            rows = pl.ds(pl.multiple_of(c * chunk, chunk), chunk)
            rows_im = pl.ds(pl.multiple_of(c * chunk + quarter_rows, chunk), chunk)
            re = [spectra_ref[0, which, s, rows, :].astype(jnp.float32) for s in range(4)]
            im = [spectra_ref[1, which, s, rows, :].astype(jnp.float32) for s in range(4)]
            a_re, b_re, c_re, d_re = re[0] + re[2], re[0] - re[2], re[1] + re[3], re[1] - re[3]
            a_im, b_im, c_im, d_im = im[0] + im[2], im[0] - im[2], im[1] + im[3], im[1] - im[3]
            parts = (
                (a_re + c_re, a_im + c_im),
                (b_re - d_im, b_im + d_re),
                (a_re - c_re, a_im - c_im),
                (b_re + d_im, b_im - d_re),
            )
            for r in range(4):
                folded[r, rows, lanes] = parts[r][0].astype(jnp.bfloat16)
                folded[r, rows_im, lanes] = parts[r][1].astype(jnp.bfloat16)

    for r in range(4):
        product = jnp.dot(table_ref[r], folded[r], preferred_element_type=jnp.float32)
        comps[2 * step, r] = product[:, :128]
        comps[2 * step + 1, r] = product[:, 128:]

    @pl.when(step == pl.num_programs(0) - 1)
    def _():
        spline_coefficients(mesh_ref, coef)
        scale = (quarter_rows * 2) ** (-0.5)

        @pl.loop(0, 4 * blocks)
        def _(index):
            block, r = index // 4, index % 4
            for v in range(padded // SUB):
                source = pl.ds(pl.multiple_of(block * padded + v * SUB, SUB), SUB)
                total, slope = spline_sums(
                    wave_ref[block, pl.ds(pl.multiple_of(r * padded + v * SUB, SUB), SUB), :],
                    lambda j: comps[j, r, source, :],
                    coef,
                    points,
                    scale,
                )
                out_ref[block, pl.ds(pl.multiple_of(r * padded + v * SUB, SUB), SUB), :] = total
                out_ref[block, pl.ds(pl.multiple_of((4 + r) * padded + v * SUB, SUB), SUB), :] = slope

        rows = quarter_rows * 4 // blocks // 4
        for block in range(blocks):
            before, after = (block - 1) % blocks, (block + 1) % blocks
            out_ref[block, 8 * padded : 8 * padded + 2, :] = out_ref[
                before, 7 * padded + rows - 2 : 7 * padded + rows, :
            ]
            out_ref[block, 8 * padded + 2 : 8 * padded + 4, :] = out_ref[
                after, 4 * padded : 4 * padded + 2, :
            ]
            out_ref[block, 8 * padded + 4 : 8 * padded + 8, :] = jnp.zeros((4, 128), jnp.float32)


def slab_sums(kernel_mesh, spectra, table, wave, blocks, padded):
    points = kernel_mesh.shape[0]
    _, comps, _, rows, lanes = spectra.shape
    out_rows = 8 * padded + 8
    return pl.pallas_call(
        functools.partial(slab_kernel, blocks, padded),
        grid=(comps // 2,),
        out_shape=jax.ShapeDtypeStruct((blocks, out_rows, lanes), jnp.float32),
        in_specs=[
            pl.BlockSpec(memory_space=pltpu.SMEM),
            pl.BlockSpec((2, 2, 4, rows, lanes), lambda i: (0, i, 0, 0, 0)),
            pl.BlockSpec(table.shape, lambda i: (0, 0, 0)),
            pl.BlockSpec(wave.shape, lambda i: (0, 0, 0)),
        ],
        out_specs=pl.BlockSpec((blocks, out_rows, lanes), lambda i: (0, 0, 0)),
        scratch_shapes=[
            pltpu.VMEM((4, 2 * rows, 2 * lanes), jnp.bfloat16),
            pltpu.VMEM((points, 4, blocks * padded, lanes), jnp.float32),
            pltpu.VMEM((5, points, SUB, 128), jnp.float32),
        ],
        compiler_params=pltpu.CompilerParams(
            dimension_semantics=("arbitrary",), vmem_limit_bytes=60 * 1024 * 1024
        ),
        cost_estimate=pl.CostEstimate(flops=2 * 10**10, bytes_accessed=2 * 10**7, transcendentals=0),
    )(kernel_mesh, spectra, table, wave)


def exchange_pairs(group, row):
    far = row < 4
    near = row % 4 < 2
    a, b, c, d = group
    a, c = jnp.where(far, a, pltpu.roll(c, 4, 0)), jnp.where(far, pltpu.roll(a, 4, 0), c)
    b, d = jnp.where(far, b, pltpu.roll(d, 4, 0)), jnp.where(far, pltpu.roll(b, 4, 0), d)
    a, b = jnp.where(near, a, pltpu.roll(b, 2, 0)), jnp.where(near, pltpu.roll(a, 6, 0), b)
    c, d = jnp.where(near, c, pltpu.roll(d, 2, 0)), jnp.where(near, pltpu.roll(c, 6, 0), d)
    return a, b, c, d


def domain_kernel(
    blocks,
    padded,
    sums_ref,
    density_ref,
    rate_ref,
    gradient_ref,
    edge_ref,
    out_ref,
    first,
    second,
    faces,
    arrived,
    send_sem,
    recv_sem,
):
    depth, height, lanes = density_ref.shape
    count = lax.axis_size("yz")
    me = lax.axis_index("yz")
    right, left = lax.rem(me + 1, count), lax.rem(me + count - 1, count)
    barrier = pltpu.get_barrier_semaphore()
    for neighbour in (left, right):
        pl.semaphore_signal(
            barrier, inc=1, device_id={"yz": neighbour}, device_id_type=pl.DeviceIdType.MESH
        )
    pl.semaphore_wait(barrier, 2)

    row = lax.broadcasted_iota(jnp.int32, (SUB, lanes), 0)
    lane = lax.broadcasted_iota(jnp.int32, (SUB, lanes), 1)
    per_class = depth // 4
    octets = height // SUB
    low_face = [jnp.zeros((SUB, lanes), jnp.float32)] * octets
    high_face = [jnp.zeros((SUB, lanes), jnp.float32)] * octets
    for octet in range(octets):
        ys = slice(octet * SUB, octet * SUB + SUB)
        for r in range(4):
            for quad in range(padded // SUB):
                totals = exchange_pairs(
                    [
                        sums_ref[4 * octet + j, r * padded + quad * SUB : r * padded + quad * SUB + SUB, :]
                        for j in range(4)
                    ],
                    row,
                )
                slopes = exchange_pairs(
                    [
                        sums_ref[
                            4 * octet + j, (4 + r) * padded + quad * SUB : (4 + r) * padded + quad * SUB + SUB, :
                        ]
                        for j in range(4)
                    ],
                    row,
                )
                for i in range(4):
                    if 4 * quad + i >= per_class:
                        continue
                    x = 4 * (4 * quad + i) + r
                    grad_scale = density_ref[x, ys, :] * slopes[i]
                    third = grad_scale * gradient_ref[2, x, ys, :]
                    onward = jnp.where(lane == lanes - 1, 0.0, pltpu.roll(third, lanes - 1, 1))
                    back = jnp.where(lane == 0, 0.0, pltpu.roll(third, 1, 1))
                    out_ref[x, ys, :] = totals[i] + rate_ref[x, ys, :] * grad_scale - 0.5 * (onward - back)
                    first[x + 1, ys, :] = grad_scale * gradient_ref[0, x, ys, :]
                    second[x, ys, :] = grad_scale * gradient_ref[1, x, ys, :]
                    low_face[octet] = jnp.where(lane == x, third[:, :1], low_face[octet])
                    high_face[octet] = jnp.where(lane == x, third[:, lanes - 1 :], high_face[octet])
        faces[0, ys, :] = low_face[octet]
        faces[1, ys, :] = high_face[octet]

    copies = []
    for side, neighbour in ((0, left), (1, right)):
        copy = pltpu.make_async_remote_copy(
            src_ref=faces.at[side],
            dst_ref=arrived.at[side],
            send_sem=send_sem.at[side],
            recv_sem=recv_sem.at[side],
            device_id={"yz": neighbour},
            device_id_type=pl.DeviceIdType.MESH,
        )
        copy.start()
        copies.append(copy)

    for octet in range(octets):
        ys = slice(octet * SUB, octet * SUB + SUB)
        for side, x in ((0, 0), (1, depth + 1)):
            edge = jnp.zeros((SUB, lanes), jnp.float32)
            for j in range(4):
                piece = sums_ref[4 * octet + j, 8 * padded : 8 * padded + SUB, :]
                shift = (2 * j - 2 * side) % SUB
                piece = pltpu.roll(piece, shift, 0) if shift else piece
                edge = jnp.where(row // 2 == j, piece, edge)
            first[x, ys, :] = edge * edge_ref[side, ys, :]

    rows_all = lax.broadcasted_iota(jnp.int32, (SUB, lanes), 0)

    @pl.loop(0, depth)
    def _(x):
        pieces = [second[x, o * SUB : o * SUB + SUB, :] for o in range(octets)]
        up = [pltpu.roll(p, SUB - 1, 0) for p in pieces]
        down = [pltpu.roll(p, 1, 0) for p in pieces]
        for o in range(octets):
            ys = slice(o * SUB, o * SUB + SUB)
            following = jnp.where(rows_all == SUB - 1, up[(o + 1) % octets], up[o])
            previous = jnp.where(rows_all == 0, down[o - 1], down[o])
            along = first[x + 2, ys, :] - first[x, ys, :]
            out_ref[x, ys, :] = out_ref[x, ys, :] - 0.5 * (along + (following - previous))

    for copy in copies:
        copy.wait()
    for o in range(octets):
        ys = slice(o * SUB, o * SUB + SUB)
        next_face, previous_face = arrived[0, ys, :], arrived[1, ys, :]
        for x in range(depth):
            edges = jnp.where(lane == lanes - 1, next_face[:, x : x + 1], 0.0) - jnp.where(
                lane == 0, previous_face[:, x : x + 1], 0.0
            )
            out_ref[x, ys, :] = out_ref[x, ys, :] - 0.5 * edges


def domain_result(sums, density, rate, gradient, edges, blocks, padded):
    depth, height, lanes = density.shape
    vmem = pl.BlockSpec(memory_space=pltpu.VMEM)
    return pl.pallas_call(
        functools.partial(domain_kernel, blocks, padded),
        out_shape=jax.ShapeDtypeStruct(density.shape, jnp.float32),
        in_specs=[vmem] * 5,
        out_specs=vmem,
        scratch_shapes=[
            pltpu.VMEM((depth + 2, height, lanes), jnp.float32),
            pltpu.VMEM((depth, height, lanes), jnp.float32),
            pltpu.VMEM((2, height, lanes), jnp.float32),
            pltpu.VMEM((2, height, lanes), jnp.float32),
            pltpu.SemaphoreType.DMA((2,)),
            pltpu.SemaphoreType.DMA((2,)),
        ],
        compiler_params=pltpu.CompilerParams(collective_id=0, has_side_effects=True),
    )(sums, density, rate, gradient, edges)


def solution(mesh):
    blocks = mesh.shape["gx"]

    def shards(spectra, kernel_mesh, density, local_wave, wave_density, wave_gradient):
        _, points, length, thin, lanes = spectra.shape
        depth, height, _ = density.shape
        per_class = depth // 4
        padded = -(-2 * per_class // SUB) * SUB
        table = jnp.asarray(split_tables(length, blocks, padded))
        forward = [(i, (i + 1) % blocks) for i in range(blocks)]
        backward = [(i, (i - 1) % blocks) for i in range(blocks)]
        product = density * wave_gradient[0]
        edges = jnp.stack(
            [
                lax.ppermute(product[-1], "gx", forward),
                lax.ppermute(product[0], "gx", backward),
            ]
        )
        wave = local_wave.reshape(per_class, 4, blocks, 2, lanes).transpose(2, 1, 0, 3, 4)
        wave = wave.reshape(blocks, 4, 2 * per_class, lanes)
        wave = lax.all_to_all(wave, "gx", split_axis=0, concat_axis=0, tiled=True)
        wave = jnp.pad(wave, ((0, 0), (0, 0), (0, padded - 2 * per_class), (0, 0)))
        wave = wave.reshape(blocks, 4 * padded, lanes)
        sums = slab_sums(
            kernel_mesh, spectra.reshape(2, points, 4, length // 2, lanes), table, wave, blocks, padded
        )
        sums = lax.all_to_all(sums, "gx", split_axis=0, concat_axis=0, tiled=True)
        return domain_result(sums, density, wave_density, wave_gradient, edges, blocks, padded)

    return jax.shard_map(
        shards,
        mesh=mesh,
        in_specs=(
            P(None, None, None, "gx", "yz"),
            P(),
            P("gx", None, "yz"),
            P("gx", None, "yz"),
            P("gx", None, "yz"),
            P(None, "gx", None, "yz"),
        ),
        out_specs=P("gx", None, "yz"),
        check_vma=False,
    )
```

time: 222 us -> 79.4 us (0.36)
  matrix products: 76.2 us -> 0 us
  other arithmetic: 49.5 us -> 1.78 us
  Pallas kernels: 0 us -> 35.8 us
  between operations: 32.9 us -> 0.05 us
  starting transfers between devices: 27.5 us -> 6.33 us
  local copies, waits for them, and re-layouts: 24.8 us -> 4.38 us
  blocking collectives: 0 us -> 16.2 us
  waiting for transfers between devices: 9.24 us -> 14.3 us
    dot_general x3 -> x0, matrix products: 76.2 us -> none  [the longest x1 32.3 us: shards(): jnp.einsum('pckyz,pkx->cxyz', spectra, tables, preferred_element_type=jnp...]
    pallas_call x0 -> x2, Pallas kernels: none -> 35.8 us  [the longest x1 25.1 us: slab_sums(): pl.pallas_call(functools.partial(slab_kernel, blocks, padded), grid=(comp...]
    all_to_all x5 -> x1, starting transfers between devices: 21.4 us -> 3.7 us  [shards(): sums = lax.all_to_all(sums, 'gx', split_axis=0, concat_axis=0, tiled=True)]
    all_to_all x0 -> x1, blocking collectives: none -> 16.2 us  [shards(): wave = lax.all_to_all(wave, 'gx', split_axis=0, concat_axis=0, tiled=True)]
    div x6 -> x0, other arithmetic: 15.1 us -> none  [the longest x1 10.6 us: spline_second(): lax.linalg.tridiagonal_solve(lower_band, main_band, upper_band, right_side)]
    add x2 -> x0, other arithmetic: 13.5 us -> none  [the longest x1 12.2 us: contract(): upper_hot = (labels == interval[None] + 1).astype(jnp.float32)]
    ppermute x4 -> x2, waiting for transfers between devices: 2.17 us -> 14.3 us  [the longest x1 11.9 us: shards(): lax.ppermute(product[0], 'gx', backward)]
    slice x10 -> x0, local copies, waits for them, and re-layouts: 9.84 us -> none  [the longest x1 2.69 us: shards(): flux_second = grad_scale * wave_gradient[1]]
  transfers between devices with their start and end apart: 9 -> 3, of which waited for: 3 -> 2; matrix products, arithmetic and copies ran while one was open for 49% -> 2% of each run, Pallas kernels for 0% -> 0%
where the time goes in v1:
time: 79.4 us; the launch traced here: 78.8 us
  Pallas kernels  35.8 us (45%)
  blocking collectives  16.2 us (20%)
  waiting for transfers between devices  14.3 us (18%)
  starting transfers between devices  6.33 us (8%)
  local copies, waits for them, and re-layouts  4.38 us (6%)
  other arithmetic  1.78 us (2%)
    pallas_call x1, Pallas kernels, slab_sums(): pl.pallas_call(functools.partial(slab_kernel, blocks, padded), grid=(comp...  25.1 us
    all_to_all x1, blocking collectives, shards(): wave = lax.all_to_all(wave, 'gx', split_axis=0, concat_axis=0, tiled=True)  16.2 us
    ppermute x1, waiting for transfers between devices, shards(): lax.ppermute(product[0], 'gx', backward)  11.9 us
    pallas_call x1, Pallas kernels, domain_result(): pl.pallas_call(functools.partial(domain_kernel, blocks, padded), out_shap...  10.7 us
    all_to_all x1, starting transfers between devices, shards(): sums = lax.all_to_all(sums, 'gx', split_axis=0, concat_axis=0, tiled=True)  3.7 us
    unnamed x5, local copies, waits for them, and re-layouts  3.05 us
    ppermute x1, starting transfers between devices, shards(): lax.ppermute(product[0], 'gx', backward)  2.62 us
    ppermute x1, waiting for transfers between devices, shards(): lax.ppermute(product[-1], 'gx', forward)  2.4 us
  transfers between devices with their start and end apart: 3, of which 2 were waited for; matrix products, arithmetic and copies ran while one was open for 2% of the time, Pallas kernels for 0%

profile of v1, /device:TPU:0, one launch (start us, length us, event | category | flops | bytes accessed | tf_op | source)
XLA Modules:
  0.0 78.8 jit_solution(6160674887809778137)
XLA Ops:
  0.0 1.3 %copy.8 = f32[8,4,20,2,128]{4,3,2,1,0:T(2,128)S(1)} copy(f32[8,4,20,2,128]{4,3,0,1,2:T(2,128)} %bitcast.15) | data formatting | bytes 1310720 | tf_op jit(solution)/shard_map/transpose | solution.py:341
  1.3 16.2 %all_to_all.10 = f32[8,4,40,128]{3,2,1,0:T(8,128)} all-to-all(f32[8,4,40,128]{3,2,1,0:T(8,128)S(1)} %bitcast.14), channel_id=1, replica_groups=mesh['gx'=8,'yz'=4] {'gx'}, dimensions={0} | all-to-all | bytes 1310720 | tf_op jit(solution)/shard_map/all_to_all | solution.py:343
  17.5 25.1 %shard_map.73 = f32[8,328,128]{2,1,0:T(8,128)} custom-call(f32[20]{0:T(128)} %mesh_ref.1, bf16[2,20,4,320,128]{4,3,2,1,0:T(8,128)(2,1)} %bitcast.19, bf16[4,320,640]{2,1,0:T(8,128)(2,1)} %constant.1.clone.table_ref, f32[8,160,128]{2,1,0:T(8,128)} %bitcast.16), custom_call_target="tpu_custom_call" | custom-call | flops 20000000000 | bytes 20000000 | tf_op jit(solution)/shard_map/pallas_call | solution.py:150
  42.7 0.0 copy-start.1
  42.7 3.7 %all-to-all-start.1 = ((f32[8,328,128]{2,1,0:T(8,128)}), f32[8,328,128]{2,1,0:T(8,128)S(1)}, u32[]{:S(2)}, u32[]{:S(2)}) async-start(f32[8,328,128]{2,1,0:T(8,128)} %shard_map.73), calls=%async_computation.1 | async-start | bytes 2686976 | tf_op jit(solution)/shard_map/all_to_all | solution.py:349
  46.4 0.0 copy-done.1
  46.4 1.2 %bitcast_multiply_fusion = f32[80,16,128]{2,1,0:T(8,128)S(1)} fusion(f32[80,16,128]{2,1,0:T(8,128)S(1)} %copy-done.1, f32[3,80,16,128]{3,2,1,0:T(8,128)} %gradient_ref.1), kind=kLoop, calls=%fused_computation | loop fusion | flops 163840 | bytes 1966080 | tf_op jit(solution)/shard_map/mul | solution.py:334
  47.6 2.6 %collective-permute-start.1 = (f32[16,128]{1,0:T(8,128)S(1)}, f32[16,128]{1,0:T(8,128)S(1)}, u32[]{:S(2)}, u32[]{:S(2)}) collective-permute-start(f32[16,128]{1,0:T(8,128)S(1)} %get-tuple-element.6), channel_id=1, source_target_pairs={{0,28},{4,0},{8,4},{12,8},{16,12},{20,16},{24,20},{28,24},{1,29},{... | collective-permute-start | bytes 24584 | tf_op jit(solution)/shard_map/ppermute | solution.py:338
  50.2 0.0 collective-permute-start
  50.2 11.9 %collective-permute-done.1 = f32[16,128]{1,0:T(8,128)S(1)} collective-permute-done((f32[16,128]{1,0:T(8,128)S(1)}, f32[16,128]{1,0:T(8,128)S(1)}, u32[]{:S(2)}, u32[]{:S(2)}) %collective-permute-start.1) | collective-permute-done | bytes 8224 | tf_op jit(solution)/shard_map/ppermute | solution.py:338
  62.1 2.4 %collective-permute-done = f32[16,128]{1,0:T(8,128)S(1)} collective-permute-done((f32[16,128]{1,0:T(8,128)S(1)}, f32[16,128]{1,0:T(8,128)S(1)}, u32[]{:S(2)}, u32[]{:S(2)}) %collective-permute-start) | collective-permute-done | bytes 8224 | tf_op jit(solution)/shard_map/ppermute | solution.py:337
  64.5 0.6 pad_maximum_fusion.edge_ref
  65.1 0.0 all-to-all-done.1.sums_ref
  65.1 0.0 copy-start
  65.1 1.1 %copy-done = f32[8,328,128]{2,1,0:T(8,128)} copy-done((f32[8,328,128]{2,1,0:T(8,128)}, f32[8,328,128]{2,1,0:T(8,128)S(1)}, u32[]{:S(2)}) %copy-start) | copy-done | bytes 1343512
  66.2 10.7 %shard_map.74 = f32[80,16,128]{2,1,0:T(8,128)} custom-call(f32[8,328,128]{2,1,0:T(8,128)} %copy-done, f32[80,16,128]{2,1,0:T(8,128)} %density_ref.1, f32[80,16,128]{2,1,0:T(8,128)} %rate_ref.1, f32[3,80,16,128]{3,2,1,0:T(8,128)} %gradient_ref.1, f32[2,16,128]{2,1,0:T(8,128)} %pad_maximum_fusion.edge_ref), custom_call_target="tpu_custom_call" | custom-call | tf_op jit(solution)/shard_map/pallas_call | solution.py:306
  76.9 2.0 %copy.10 = f32[80,16,128]{2,1,0:T(8,128)} copy(f32[80,16,128]{2,1,0:T(8,128)} %shard_map.74) | data formatting | bytes 1310720
  (1 shorter events, 0.0 us)
Async XLA Ops:
  42.7 3.7 %copy-start.1 = (f32[80,16,128]{2,1,0:T(8,128)S(1)}, f32[80,16,128]{2,1,0:T(8,128)}, u32[]{:S(2)}) copy-start(f32[80,16,128]{2,1,0:T(8,128)} %density_ref.1) | copy-start | bytes 1966084
  42.7 22.4 %all-to-all-start.1 = ((f32[8,328,128]{2,1,0:T(8,128)}), f32[8,328,128]{2,1,0:T(8,128)S(1)}, u32[]{:S(2)}, u32[]{:S(2)}) async-start(f32[8,328,128]{2,1,0:T(8,128)} %shard_map.73), calls=%async_computation.1 | async-start | bytes 2686976 | tf_op jit(solution)/shard_map/all_to_all | solution.py:349
  47.6 14.5 %collective-permute-start.1 = (f32[16,128]{1,0:T(8,128)S(1)}, f32[16,128]{1,0:T(8,128)S(1)}, u32[]{:S(2)}, u32[]{:S(2)}) collective-permute-start(f32[16,128]{1,0:T(8,128)S(1)} %get-tuple-element.6), channel_id=1, source_target_pairs={{0,28},{4,0},{8,4},{12,8},{16,12},{20,16},{24,20},{28,24},{1,29},{... | collective-permute-start | bytes 24584 | tf_op jit(solution)/shard_map/ppermute | solution.py:338
  50.2 14.3 %collective-permute-start = (f32[16,128]{1,0:T(8,128)S(1)}, f32[16,128]{1,0:T(8,128)S(1)}, u32[]{:S(2)}, u32[]{:S(2)}) collective-permute-start(f32[16,128]{1,0:T(8,128)S(1)} %get-tuple-element.5), channel_id=1, source_target_pairs={{0,4},{4,8},{8,12},{12,16},{16,20},{20,24},{24,28},{28,0},{1,5},{5... | collective-permute-start | bytes 24584 | tf_op jit(solution)/shard_map/ppermute | solution.py:337
  65.1 1.1 %copy-start = (f32[8,328,128]{2,1,0:T(8,128)}, f32[8,328,128]{2,1,0:T(8,128)S(1)}, u32[]{:S(2)}) copy-start(f32[8,328,128]{2,1,0:T(8,128)S(1)} %all-to-all-done.1.sums_ref) | copy-start | bytes 4030468

commit v2 on v0

v2 whole, which is shorter than its diff:
```python
import functools
import math

import jax
import jax.numpy as jnp
import numpy as np
from jax import lax
from jax.experimental import pallas as pl
from jax.experimental.pallas import tpu as pltpu
from jax.sharding import PartitionSpec as P

SUB = 8


def split_tables(length, blocks, padded_rows):
    quarter = length // 4
    per_block = length // blocks // 4
    out = np.zeros((4, blocks, padded_rows, 2, quarter, 2), np.float32)
    k = np.arange(quarter)
    for r in range(4):
        m = np.arange(blocks * per_block).reshape(blocks, per_block)
        x = 4 * m + r
        phases = (x[..., None] * k) % length
        angles = phases.astype(np.float32) * np.float32(2.0 * math.pi / length)
        pair = np.stack([np.cos(angles), -np.sin(angles)], axis=2)
        for y in range(2):
            out[r, :, y : 2 * per_block : 2, :, :, y] = pair
    flat = out.reshape(4, blocks * padded_rows, 4 * quarter)
    return flat.astype(jnp.bfloat16)


def spline_coefficients(mesh_ref, coef_ref):
    points = mesh_ref.shape[0]
    ones = jnp.ones((SUB, 128), jnp.float32)
    node = [ones * mesh_ref[j] for j in range(points)]
    gap = [node[j + 1] - node[j] for j in range(points - 1)]
    carry = jnp.zeros((SUB, 128), jnp.float32)
    for j in range(points):
        coef_ref[0, j] = node[j]
        if j < points - 1:
            coef_ref[1, j] = 1.0 / gap[j]
        if 1 <= j < points - 1:
            pivot = 1.0 / (2.0 * (gap[j - 1] + gap[j]) - gap[j - 1] * carry)
            carry = gap[j] * pivot
            coef_ref[2, j] = pivot
            coef_ref[3, j] = gap[j - 1] * pivot
            coef_ref[4, j] = carry


def spline_sums(wave, value_of, coef_ref, points, scale):
    values = [value_of(j) for j in range(points)]
    forward = [None] * points
    slope_before = (values[1] - values[0]) * coef_ref[1, 0]
    for j in range(1, points - 1):
        slope_here = (values[j + 1] - values[j]) * coef_ref[1, j]
        term = (slope_here - slope_before) * coef_ref[2, j]
        if j > 1:
            term = term - coef_ref[3, j] * forward[j - 1]
        forward[j] = term
        slope_before = slope_here
    zero = jnp.zeros_like(wave)
    sixth = [zero] * points
    for j in range(points - 2, 0, -1):
        sixth[j] = forward[j] if j == points - 2 else forward[j] - coef_ref[4, j] * sixth[j + 1]
    picked = [values[0], values[1], sixth[0], sixth[1], coef_ref[0, 0], coef_ref[0, 1]]
    for j in range(1, points - 1):
        above = wave >= coef_ref[0, j]
        here = [values[j], values[j + 1], sixth[j], sixth[j + 1], coef_ref[0, j], coef_ref[0, j + 1]]
        picked = [jnp.where(above, new, old) for new, old in zip(here, picked)]
    value_low, value_high, sixth_low, sixth_high, low, high = picked
    width = high - low
    inverse = 1.0 / width
    a = (high - wave) * inverse
    b = (wave - low) * inverse
    square_a, square_b = a * a, b * b
    bent = ((square_a * a - a) * sixth_low + (square_b * b - b) * sixth_high) * (width * width)
    total = a * value_low + b * value_high + bent
    turn = ((3.0 * square_b - 1.0) * sixth_high - (3.0 * square_a - 1.0) * sixth_low) * width
    slope = (value_high - value_low) * inverse + turn
    return total * scale, slope * scale


def exchange_pairs(group, row):
    far = row < 4
    near = row % 4 < 2
    a, b, c, d = group
    a, c = jnp.where(far, a, pltpu.roll(c, 4, 0)), jnp.where(far, pltpu.roll(a, 4, 0), c)
    b, d = jnp.where(far, b, pltpu.roll(d, 4, 0)), jnp.where(far, pltpu.roll(b, 4, 0), d)
    a, b = jnp.where(near, a, pltpu.roll(b, 2, 0)), jnp.where(near, pltpu.roll(a, 6, 0), b)
    c, d = jnp.where(near, c, pltpu.roll(d, 2, 0)), jnp.where(near, pltpu.roll(c, 6, 0), d)
    return a, b, c, d


def fold_parts(spectra_ref, folded, which, rows, rows_im):
    lanes = slice(which * 128, which * 128 + 128)
    re = [spectra_ref[0, which, s, rows, :].astype(jnp.float32) for s in range(4)]
    im = [spectra_ref[1, which, s, rows, :].astype(jnp.float32) for s in range(4)]
    a_re, b_re, c_re, d_re = re[0] + re[2], re[0] - re[2], re[1] + re[3], re[1] - re[3]
    a_im, b_im, c_im, d_im = im[0] + im[2], im[0] - im[2], im[1] + im[3], im[1] - im[3]
    parts = (
        (a_re + c_re, a_im + c_im),
        (b_re - d_im, b_im + d_re),
        (a_re - c_re, a_im - c_im),
        (b_re + d_im, b_im - d_re),
    )
    for r in range(4):
        folded[r, rows, lanes] = parts[r][0].astype(jnp.bfloat16)
        folded[r, rows_im, lanes] = parts[r][1].astype(jnp.bfloat16)


def push(source, target, send_sem, recv_sem, axis, index):
    return pltpu.make_async_remote_copy(
        src_ref=source,
        dst_ref=target,
        send_sem=send_sem,
        recv_sem=recv_sem,
        device_id={axis: index},
        device_id_type=pl.DeviceIdType.MESH,
    )


def whole_kernel(
    padded,
    mesh_ref,
    spectra_ref,
    table_ref,
    wave_ref,
    density_ref,
    rate_ref,
    gradient_ref,
    out_ref,
    folded,
    comps,
    coef,
    wave_out,
    wave_in,
    sums_out,
    sums_in,
    rim_out,
    rim_in,
    edge_out,
    edge_in,
    first,
    second,
    faces,
    arrived,
    wave_send,
    wave_recv,
    sums_send,
    sums_recv,
    rim_send,
    rim_recv,
    edge_send,
    edge_recv,
    face_send,
    face_recv,
):
    step = pl.program_id(0)
    points = mesh_ref.shape[0]
    quarter_rows = spectra_ref.shape[3]
    depth, height, lanes = density_ref.shape
    per_class = depth // 4
    octets = height // SUB
    blocks = lax.axis_size("gx")
    me = lax.axis_index("gx")
    count = lax.axis_size("yz")
    place = lax.axis_index("yz")
    right, left = lax.rem(place + 1, count), lax.rem(place + count - 1, count)
    after, before = lax.rem(me + 1, blocks), lax.rem(me + blocks - 1, blocks)
    row = lax.broadcasted_iota(jnp.int32, (SUB, lanes), 0)
    lane = lax.broadcasted_iota(jnp.int32, (SUB, lanes), 1)
    edge_copies = [
        push(edge_out.at[0], edge_in.at[0], edge_send.at[0], edge_recv.at[0], "gx", after),
        push(edge_out.at[1], edge_in.at[1], edge_send.at[1], edge_recv.at[1], "gx", before),
    ]

    def to_peer(out, landing, send_sem, recv_sem, peer):
        return push(out.at[peer], landing.at[me], send_sem.at[peer], recv_sem.at[me], "gx", peer)

    def from_peer(out, landing, send_sem, recv_sem, peer):
        return push(out.at[peer], landing.at[peer], send_sem.at[peer], recv_sem.at[peer], "gx", peer)

    waves = (wave_out, wave_in, wave_send, wave_recv)
    sums = (sums_out, sums_in, sums_send, sums_recv)
    rims = (rim_out, rim_in, rim_send, rim_recv)

    @pl.when(step == 0)
    def _():
        barrier = pltpu.get_barrier_semaphore()

        @pl.loop(1, blocks)
        def _(i):
            pl.semaphore_signal(
                barrier, 1, device_id={"gx": lax.rem(me + i, blocks)}, device_id_type=pl.DeviceIdType.MESH
            )

        for neighbour in (left, right):
            pl.semaphore_signal(
                barrier, 1, device_id={"yz": neighbour}, device_id_type=pl.DeviceIdType.MESH
            )
        for octet in range(octets):
            ys = slice(octet * SUB, octet * SUB + SUB)
            for r in range(4):
                for quad in range(padded // SUB):
                    group = [
                        wave_ref[min(4 * (4 * quad + i), depth - 4) + r, ys, :] for i in range(4)
                    ]
                    moved = exchange_pairs(group, row)
                    start = r * padded + quad * SUB
                    for j in range(4):
                        wave_out[4 * octet + j, start : start + SUB, :] = moved[j]
        edge_out[0] = density_ref[depth - 1] * gradient_ref[0, depth - 1]
        edge_out[1] = density_ref[0] * gradient_ref[0, 0]
        pl.semaphore_wait(barrier, blocks + 1)

        @pl.loop(1, blocks)
        def _(i):
            to_peer(*waves, lax.rem(me + i, blocks)).start()

        for copy in edge_copies:
            copy.start()
        wave_in[me] = wave_out[me]

    chunk = 32
    for which in range(2):

        @pl.loop(0, quarter_rows // chunk)
        def _(c):
            rows = pl.ds(pl.multiple_of(c * chunk, chunk), chunk)
            rows_im = pl.ds(pl.multiple_of(c * chunk + quarter_rows, chunk), chunk)
            fold_parts(spectra_ref, folded, which, rows, rows_im)

    for r in range(4):
        product = jnp.dot(table_ref[r], folded[r], preferred_element_type=jnp.float32)
        comps[2 * step, r] = product[:, :128]
        comps[2 * step + 1, r] = product[:, 128:]

    @pl.when(step == pl.num_programs(0) - 1)
    def _():
        spline_coefficients(mesh_ref, coef)
        scale = (quarter_rows * 2) ** (-0.5)

        @pl.loop(1, blocks)
        def _(i):
            from_peer(*waves, lax.rem(me + i, blocks)).wait_recv()

        @pl.loop(1, blocks + 1)
        def _(i):
            block = lax.rem(me + i, blocks)

            @pl.loop(0, 4)
            def _(r):
                for v in range(padded // SUB):
                    source = pl.ds(pl.multiple_of(block * padded + v * SUB, SUB), SUB)
                    low = pl.ds(pl.multiple_of(r * padded + v * SUB, SUB), SUB)
                    high = pl.ds(pl.multiple_of((4 + r) * padded + v * SUB, SUB), SUB)
                    total, slope = spline_sums(
                        wave_in[block, low, :], lambda j: comps[j, r, source, :], coef, points, scale
                    )
                    sums_out[block, low, :] = total
                    sums_out[block, high, :] = slope

            @pl.when(i < blocks)
            def _():
                to_peer(*sums, block).start()

        filled = 2 * per_class
        for block in range(blocks):
            rim_out[block, 0:2, :] = sums_out[
                (block - 1) % blocks, 7 * padded + filled - 2 : 7 * padded + filled, :
            ]
            rim_out[block, 2:4, :] = sums_out[(block + 1) % blocks, 4 * padded : 4 * padded + 2, :]
            rim_out[block, 4:8, :] = jnp.zeros((4, 128), jnp.float32)

        @pl.loop(1, blocks)
        def _(i):
            to_peer(*rims, lax.rem(me + i, blocks)).start()

        sums_in[me] = sums_out[me]
        rim_in[me] = rim_out[me]

        @pl.loop(1, blocks)
        def _(i):
            from_peer(*sums, lax.rem(me + blocks - i, blocks)).wait_recv()

        low_face = [jnp.zeros((SUB, lanes), jnp.float32)] * octets
        high_face = [jnp.zeros((SUB, lanes), jnp.float32)] * octets
        for octet in range(octets):
            ys = slice(octet * SUB, octet * SUB + SUB)
            for r in range(4):
                for quad in range(padded // SUB):
                    low, high = r * padded + quad * SUB, (4 + r) * padded + quad * SUB
                    totals = exchange_pairs(
                        [sums_in[4 * octet + j, low : low + SUB, :] for j in range(4)], row
                    )
                    slopes = exchange_pairs(
                        [sums_in[4 * octet + j, high : high + SUB, :] for j in range(4)], row
                    )
                    for i in range(4):
                        if 4 * quad + i >= per_class:
                            continue
                        x = 4 * (4 * quad + i) + r
                        grad_scale = density_ref[x, ys, :] * slopes[i]
                        third = grad_scale * gradient_ref[2, x, ys, :]
                        onward = jnp.where(lane == lanes - 1, 0.0, pltpu.roll(third, lanes - 1, 1))
                        back = jnp.where(lane == 0, 0.0, pltpu.roll(third, 1, 1))
                        out_ref[x, ys, :] = (
                            totals[i] + rate_ref[x, ys, :] * grad_scale - 0.5 * (onward - back)
                        )
                        first[x + 1, ys, :] = grad_scale * gradient_ref[0, x, ys, :]
                        second[x, ys, :] = grad_scale * gradient_ref[1, x, ys, :]
                        low_face[octet] = jnp.where(lane == x, third[:, :1], low_face[octet])
                        high_face[octet] = jnp.where(lane == x, third[:, lanes - 1 :], high_face[octet])
            faces[0, ys, :] = low_face[octet]
            faces[1, ys, :] = high_face[octet]

        face_copies = [
            push(faces.at[side], arrived.at[side], face_send.at[side], face_recv.at[side], "yz", neighbour)
            for side, neighbour in ((0, left), (1, right))
        ]
        for copy in face_copies:
            copy.start()

        @pl.loop(1, blocks)
        def _(i):
            from_peer(*rims, lax.rem(me + i, blocks)).wait_recv()

        for copy in edge_copies:
            copy.wait()
        for octet in range(octets):
            ys = slice(octet * SUB, octet * SUB + SUB)
            for side, x in ((0, 0), (1, depth + 1)):
                edge = jnp.zeros((SUB, lanes), jnp.float32)
                for j in range(4):
                    piece = rim_in[4 * octet + j]
                    shift = (2 * j - 2 * side) % SUB
                    piece = pltpu.roll(piece, shift, 0) if shift else piece
                    edge = jnp.where(row // 2 == j, piece, edge)
                first[x, ys, :] = edge * edge_in[side, ys, :]

        @pl.loop(0, depth)
        def _(x):
            pieces = [second[x, o * SUB : o * SUB + SUB, :] for o in range(octets)]
            up = [pltpu.roll(p, SUB - 1, 0) for p in pieces]
            down = [pltpu.roll(p, 1, 0) for p in pieces]
            for o in range(octets):
                ys = slice(o * SUB, o * SUB + SUB)
                following = jnp.where(row == SUB - 1, up[(o + 1) % octets], up[o])
                previous = jnp.where(row == 0, down[o - 1], down[o])
                along = first[x + 2, ys, :] - first[x, ys, :]
                out_ref[x, ys, :] = out_ref[x, ys, :] - 0.5 * (along + (following - previous))

        for copy in face_copies:
            copy.wait()
        for o in range(octets):
            ys = slice(o * SUB, o * SUB + SUB)
            next_face, previous_face = arrived[0, ys, :], arrived[1, ys, :]
            for x in range(depth):
                edges = jnp.where(lane == lanes - 1, next_face[:, x : x + 1], 0.0) - jnp.where(
                    lane == 0, previous_face[:, x : x + 1], 0.0
                )
                out_ref[x, ys, :] = out_ref[x, ys, :] - 0.5 * edges

        @pl.loop(1, blocks)
        def _(i):
            peer = lax.rem(me + i, blocks)
            to_peer(*waves, peer).wait_send()
            to_peer(*sums, peer).wait_send()
            to_peer(*rims, peer).wait_send()


def solution(mesh):
    blocks = mesh.shape["gx"]

    def shards(spectra, kernel_mesh, density, local_wave, wave_density, wave_gradient):
        _, points, length, thin, lanes = spectra.shape
        depth, height, _ = density.shape
        padded = -(-2 * (depth // 4) // SUB) * SUB
        rows = length // 4 * thin
        table = jnp.asarray(split_tables(length, blocks, padded))
        spectra = spectra.reshape(2, points, 4, rows, lanes)

        def fixed(array):
            zeros = (0,) * array.ndim
            return pl.BlockSpec(array.shape, lambda i: zeros)

        def real(*shape):
            return pltpu.VMEM(shape, jnp.float32)

        many = pltpu.SemaphoreType.DMA((blocks,))
        pair = pltpu.SemaphoreType.DMA((2,))
        return pl.pallas_call(
            functools.partial(whole_kernel, padded),
            grid=(points // 2,),
            out_shape=jax.ShapeDtypeStruct(density.shape, jnp.float32),
            in_specs=[
                pl.BlockSpec(memory_space=pltpu.SMEM),
                pl.BlockSpec((2, 2, 4, rows, lanes), lambda i: (0, i, 0, 0, 0)),
                fixed(table),
                fixed(local_wave),
                fixed(density),
                fixed(wave_density),
                fixed(wave_gradient),
            ],
            out_specs=fixed(density),
            scratch_shapes=[
                pltpu.VMEM((4, 2 * rows, 2 * lanes), jnp.bfloat16),
                real(points, 4, blocks * padded, lanes),
                real(5, points, SUB, lanes),
                real(blocks, 4 * padded, lanes),
                real(blocks, 4 * padded, lanes),
                real(blocks, 8 * padded, lanes),
                real(blocks, 8 * padded, lanes),
                real(blocks, SUB, lanes),
                real(blocks, SUB, lanes),
                real(2, height, lanes),
                real(2, height, lanes),
                real(depth + 2, height, lanes),
                real(depth, height, lanes),
                real(2, height, lanes),
                real(2, height, lanes),
            ]
            + [many] * 6
            + [pair] * 4,
            compiler_params=pltpu.CompilerParams(
                collective_id=0,
                has_side_effects=True,
                dimension_semantics=("arbitrary",),
                vmem_limit_bytes=60 * 1024 * 1024,
            ),
        )(kernel_mesh, spectra, table, local_wave, density, wave_density, wave_gradient)

    return jax.shard_map(
        shards,
        mesh=mesh,
        in_specs=(
            P(None, None, None, "gx", "yz"),
            P(),
            P("gx", None, "yz"),
            P("gx", None, "yz"),
            P("gx", None, "yz"),
            P(None, "gx", None, "yz"),
        ),
        out_specs=P("gx", None, "yz"),
        check_vma=False,
    )
```

time: 222 us -> 47 us (0.21)
  the two profiles are of different devices: /device:TPU:0 before, /device:TPU:7 now
where the time goes in v2:
time: 47 us; the launch traced here: 46.6 us
  Pallas kernels  44.6 us (95%)
  local copies, waits for them, and re-layouts  1.97 us (4%)
    pallas_call x1, Pallas kernels, shards(): pl.pallas_call(functools.partial(whole_kernel, padded), grid=(points // 2...  44.6 us
    unnamed x1, local copies, waits for them, and re-layouts  1.97 us

profile of v2, /device:TPU:7, one launch (start us, length us, event | category | flops | bytes accessed | tf_op | source)
XLA Modules:
  0.0 46.6 jit_solution(16845214719838966139)
XLA Ops:
  0.0 44.6 %shard_map.73 = f32[80,16,128]{2,1,0:T(8,128)} custom-call(f32[20]{0:T(128)} %mesh_ref.1, bf16[2,20,4,320,128]{4,3,2,1,0:T(8,128)(2,1)} %bitcast.1, bf16[4,320,640]{2,1,0:T(8,128)(2,1)} %constant.2.clone.table_ref, f32[80,16,128]{2,1,0:T(8,128)} %wave_ref.1, f32[80,16,128]{2,1,0:T(8,128)} %density_ref.1, f32[80,16,128]{2,1,0:T(8,128)} %rate_ref.1, ...), custom_call_target="tpu_custom_call" | custom-call | tf_op jit(solution)/shard_map/pallas_call | solution.py:392
  44.6 2.0 %copy.9 = f32[80,16,128]{2,1,0:T(8,128)} copy(f32[80,16,128]{2,1,0:T(8,128)} %shard_map.73) | data formatting | bytes 1310720

commit v3 on v2

--- a/solution.py
+++ b/solution.py
@@ -117,6 +117,25 @@
         device_id={axis: index},
         device_id_type=pl.DeviceIdType.MESH,
     )
+
+
+def peer_order(blocks):
+    masks = sorted(range(1, blocks), key=lambda m: (-bin(m // 2).count("1"), m % 2, m))
+    return masks + [0]
+
+
+def peer_at(me, blocks, i):
+    if blocks & (blocks - 1):
+        return lax.rem(me + i, blocks)
+    mask = 0
+    for turn, value in enumerate(peer_order(blocks)):
+        mask = mask + jnp.where(i == turn + 1, value, 0)
+    peer = me
+    bit = 1
+    while bit < blocks:
+        peer = peer + ((mask // bit) % 2) * bit * (1 - 2 * ((me // bit) % 2))
+        bit *= 2
+    return peer
 
 
 def whole_kernel(
@@ -215,7 +234,7 @@
 
         @pl.loop(1, blocks)
         def _(i):
-            to_peer(*waves, lax.rem(me + i, blocks)).start()
+            to_peer(*waves, peer_at(me, blocks, i)).start()
 
         for copy in edge_copies:
             copy.start()
@@ -246,7 +265,7 @@
 
         @pl.loop(1, blocks + 1)
         def _(i):
-            block = lax.rem(me + i, blocks)
+            block = peer_at(me, blocks, i)
 
             @pl.loop(0, 4)
             def _(r):

time: 47 us -> 47.6 us (1.013)
  the two profiles are of different devices: /device:TPU:7 before, /device:TPU:0 now
where the time goes in v3:
time: 47.6 us; the launch traced here: 47.3 us
  Pallas kernels  45.3 us (95%)
  local copies, waits for them, and re-layouts  1.97 us (4%)
    pallas_call x1, Pallas kernels, shards(): pl.pallas_call(functools.partial(whole_kernel, padded), grid=(points // 2...  45.3 us
    unnamed x1, local copies, waits for them, and re-layouts  1.97 us

profile of v3, /device:TPU:0, one launch (start us, length us, event | category | flops | bytes accessed | tf_op | source)
XLA Modules:
  0.0 47.3 jit_solution(15001374667645387025)
XLA Ops:
  0.0 45.3 %shard_map.73 = f32[80,16,128]{2,1,0:T(8,128)} custom-call(f32[20]{0:T(128)} %mesh_ref.1, bf16[2,20,4,320,128]{4,3,2,1,0:T(8,128)(2,1)} %bitcast.1, bf16[4,320,640]{2,1,0:T(8,128)(2,1)} %constant.2.clone.table_ref, f32[80,16,128]{2,1,0:T(8,128)} %wave_ref.1, f32[80,16,128]{2,1,0:T(8,128)} %density_ref.1, f32[80,16,128]{2,1,0:T(8,128)} %rate_ref.1, ...), custom_call_target="tpu_custom_call" | custom-call | tf_op jit(solution)/shard_map/pallas_call | solution.py:411
  45.3 2.0 %copy.9 = f32[80,16,128]{2,1,0:T(8,128)} copy(f32[80,16,128]{2,1,0:T(8,128)} %shard_map.73) | data formatting | bytes 1310720
